TPU v7x, 256 devices: a whole 4x4x8 slice. The times are simulated.
256 devices in a mesh: genome: 32 (over x, z), samples: 8 (over y, core).
Axes of the slice: x: 4, y: 4, z: 8, core: 2. Of those that a mesh axis runs over, the one named last changes fastest.
Arguments:
- genotypes: int32 [8192, 49152], P('samples', 'genome'), may hold values from 0 to 2
- residuals: bfloat16 [8192, 64], P('samples'), may hold values from -78 to 78
- variant_class: int32 [49152], P('genome'), may hold values from 0 to 7
- class_weight: float32 [8], replicated, may hold values from 0.25 to 4
- gene_start: int32 [4096], P(('genome', 'samples')), may hold values from 0 to 49151, as said below
- gene_end: int32 [4096], P(('genome', 'samples')), may hold values from 1 to 49152, as said below
Outputs:
- score_track: float32 [49152, 64], P(('genome', 'samples'))
- gene_stat: float32 [4096, 64], P(('genome', 'samples'))
Inputs may be any that keep to these rules, and one draw needn't show every extreme that they name: gene_end[g] - 1 lies in [k * 192, (k + 1) * 192) with k = g // 16. 1 <= gene_end[g] - gene_start[g] <= 192.
All inputs are finite; a program needn't handle non-finite values.
Results may differ from a plain program's by a relative error of at most 0.0003.
Values sent between devices are 32-bit elements; how exact they have to be, the bound alone decides.
A program may use at most 64 MiB of HBM per device.

v0:
```python
import jax
import jax.numpy as jnp
from jax import lax
from jax.sharding import PartitionSpec as P


def total_of_pieces(x, axis):
    blocks = lax.all_gather(x, axis)
    return blocks.sum(axis=0)


def from_everyone(x, axis):
    peers = lax.axis_size(axis)
    return lax.all_to_all(jnp.broadcast_to(x[None], (peers, *x.shape)), axis, 0, 0, tiled=True)


def collected_together(x, axis):
    leaves = jax.tree.leaves(x)
    turns = sorted(range(len(leaves)), key=lambda k: -leaves[k].size)
    width = (1, *leaves[turns[0]].shape)[-1]
    lines = [
        jnp.pad(leaves[k].reshape(-1), (0, -leaves[k].size % width)).reshape(-1, width)
        for k in turns
    ]
    both, at, found = (from_everyone(jnp.concatenate(lines), axis), 0, {})
    for k, line in zip(turns, lines):
        piece = both[:, at : at + len(line)].reshape(len(both), -1)
        found[k] = piece[:, : leaves[k].size].reshape(-1, *leaves[k].shape)
        at += len(line)
    numbers = iter(range(len(leaves)))
    return jax.tree.map(lambda _: found[next(numbers)], x)


def combined_pairwise(pieces, combine):
    while len(jax.tree.leaves(pieces)[0]) > 1:
        pieces = jax.vmap(combine)(
            *(jax.tree.map(lambda part: part[side::2], pieces) for side in (0, 1))
        )
    return jax.tree.map(lambda part: part[0], pieces)


def entering(x, axis, combine, identity):
    peers, place = (lax.axis_size(axis), lax.axis_index(axis))
    passed = jnp.arange(peers) < place

    def kept(part, zero, own):
        part = jnp.where(
            passed.reshape(-1, *(1 for _ in own.shape)), part, jnp.asarray(zero, own.dtype)
        )
        return part

    pieces = collected_together(x, axis)
    return combined_pairwise(jax.tree.map(kept, pieces, identity, x), combine)


def passed_along(value, axis, steps):
    count = lax.axis_size(axis)
    leading, last = (max(0, -steps), min(count, count - steps))
    return lax.ppermute(value, axis, [(source, source + steps) for source in range(leading, last)])


def add_pairs(earlier, later):
    return (earlier[0] + later[0], earlier[1] + later[1])


def prefix_rows(values):
    rows, columns = values.shape
    block_width = 128
    block_count = rows // block_width
    positions = jnp.arange(block_width)
    lower_ones = (positions[:, None] >= positions[None, :]).astype(jnp.float32)
    blocks = values.reshape(block_count, block_width, columns)
    inner_sums = jnp.einsum("ij,bjk->bik", lower_ones, blocks, precision=lax.Precision.HIGHEST)
    totals = inner_sums[:, -1, :]
    before = jnp.cumsum(totals, axis=0) - totals
    return (inner_sums + before[:, None, :]).reshape(rows, columns)


def local(genotypes, residuals, variant_class, class_weight, gene_start, gene_end):
    groups = lax.axis_size("samples")
    genome_count = lax.axis_size("genome")
    sample_rows, block_vars = genotypes.shape
    phenos = residuals.shape[1]
    share_rows = block_vars // groups
    total_samples = sample_rows * groups
    total_vars = block_vars * genome_count
    sample_part = lax.axis_index("samples")
    flat_index = lax.axis_index("genome") * groups + sample_part
    contract = (((0,), (0,)), ((), ()))
    dosage = genotypes.astype(jnp.bfloat16)
    partial_value = lax.dot_general(dosage, residuals, contract, preferred_element_type=jnp.float32)
    squared = lax.dot_general(
        dosage * dosage,
        jnp.ones((sample_rows,), jnp.bfloat16),
        contract,
        preferred_element_type=jnp.float32,
    )
    spread_local = jnp.sum(jnp.square(residuals.astype(jnp.float32)), axis=0)
    carry_zero = (jnp.zeros((phenos,), jnp.float32), jnp.zeros((), jnp.float32))
    summed, counts, spread_sum = (
        total_of_pieces(partial_value, "samples"),
        total_of_pieces(squared, "samples"),
        total_of_pieces(spread_local, "samples"),
    )
    classes = jnp.arange(class_weight.shape[0], dtype=jnp.int32)
    weight = jnp.sum(
        jnp.where(variant_class[:, None] == classes[None, :], class_weight[None, :], 0.0), axis=1
    )
    scores = summed * weight[:, None] * total_samples ** (-0.5)
    quad_terms = weight * weight * counts / total_samples
    local_prefix = prefix_rows(scores)
    local_quad = prefix_rows(quad_terms[:, None])[:, 0]
    ends = (local_prefix[-1], local_quad[-1])
    carry_sum, carry_quad = entering(ends, "genome", add_pairs, carry_zero)
    full_prefix = local_prefix + carry_sum[None, :]
    source, quad_source = (local_prefix, local_quad)
    last_rows = source[block_vars - share_rows :]
    last_quad = quad_source[block_vars - share_rows :]
    incoming, incoming_quad = passed_along((last_rows, last_quad), "genome", 1)
    incoming = incoming - incoming[-1][None, :]
    incoming_quad = incoming_quad - incoming_quad[-1]
    near_start = jnp.maximum(sample_part - 1, 0) * share_rows
    own_start = sample_part * share_rows
    near_rows = lax.dynamic_slice_in_dim(source, near_start, share_rows, 0)
    near_quad = lax.dynamic_slice_in_dim(quad_source, near_start, share_rows, 0)
    at_first = sample_part == 0
    prior_rows = jnp.where(at_first, incoming, near_rows)
    prior_quad = jnp.where(at_first, incoming_quad, near_quad)
    own_rows = lax.dynamic_slice_in_dim(source, own_start, share_rows, 0)
    own_quad = lax.dynamic_slice_in_dim(quad_source, own_start, share_rows, 0)
    track_rows = lax.dynamic_slice_in_dim(full_prefix, own_start, share_rows, 0)
    window = jnp.concatenate([prior_rows, own_rows], axis=0)
    quad_window = jnp.concatenate([prior_quad, own_quad], axis=0)
    window_base = (flat_index - 1) * share_rows
    positions = jnp.arange(2 * share_rows, dtype=jnp.int32)
    end_pos = gene_end - 1 - window_base
    start_pos = gene_start - 1 - window_base
    picker = (positions[None, :] == end_pos[:, None]).astype(jnp.float32) - (
        positions[None, :] == start_pos[:, None]
    ).astype(jnp.float32)
    gene_score = jnp.dot(
        picker, window, precision=lax.Precision.HIGHEST, preferred_element_type=jnp.float32
    )
    gene_quad = jnp.dot(
        picker, quad_window, precision=lax.Precision.HIGHEST, preferred_element_type=jnp.float32
    )
    variance = spread_sum / total_samples + 1e-05
    gene_stat = jnp.square(gene_score) / (variance[None, :] * (gene_quad[:, None] + 1.0))
    return (track_rows * total_vars ** (-0.5), gene_stat)


def solution(mesh):
    return jax.shard_map(
        local,
        mesh=mesh,
        in_specs=(
            P("samples", "genome"),
            P("samples", None),
            P("genome"),
            P(),
            P(("genome", "samples")),
            P(("genome", "samples")),
        ),
        out_specs=(P(("genome", "samples"), None), P(("genome", "samples"), None)),
        check_vma=False,
    )
```

profile of v0, /device:TPU:6, one launch (start us, length us, event | category | flops | bytes accessed | tf_op | source)
XLA Modules:
  0.0 87.8 jit_solution(3635893763663421555)
XLA Ops:
  7.2 0.0 all-gather.6.cloned.1.call-start
  7.2 4.3 %fusion.6 = f32[1536,64]{0,1:T(8,128)} fusion(bf16[1024,64]{0,1:T(8,128)(2,1)} %param.7, s32[1024,1536]{1,0:T(8,128)} %param.6), kind=kOutput, calls=%fused_computation.5 | convolution fusion | flops 202899456 | bytes 6815744 | tf_op jit(solution)/shard_map/dot_general | solution.py:91
  11.5 0.0 all-gather.6.cloned.1.call-update
  11.5 0.0 copy-start.1
  11.5 0.0 copy-start.2
  11.5 0.0 copy-start.5
  11.5 0.0 copy-start
  11.6 0.0 copy-start.3
  11.6 0.0 copy-start.4
  11.6 3.5 %fusion.2 = f32[1,1,1536]{2,1,0:T(1,128)S(1)} fusion(s32[1024,1536]{1,0:T(8,128)} %param.6), kind=kOutput, calls=%fused_computation.3 | convolution fusion | flops 6291456 | bytes 6297600 | tf_op jit(solution)/shard_map/dot_general | solution.py:92
  15.1 13.3 %all-gather.3 = f32[8,1,1536]{2,1,0:T(1,128)S(1)} all-gather(f32[1,1,1536]{2,1,0:T(1,128)S(1)} %fusion.2), channel_id=3, replica_groups=mesh['genome'=32,'samples'=8] {'samples'}, dimensions={0}, use_global_device_ids=true | all-gather | bytes 55296 | tf_op jit(solution)/shard_map/all_gather | solution.py:8
  28.4 0.0 copy-done.1
  28.5 0.0 copy-done.2
  28.5 0.1 select_reduce_fusion
  28.6 0.1 fusion.15
  28.7 0.1 slice.80
  28.8 0.1 reduce_window_sum.23
  28.9 0.2 subtract_reduce_fusion
  29.0 0.1 add_bitcast_fusion.1
  29.1 0.1 slice.85
  29.2 3.8 %collective-permute-start.1 = (f32[192]{0:T(256)S(1)}, f32[192]{0:T(256)S(1)}, u32[]{:S(2)}, u32[]{:S(2)}) collective-permute-start(f32[192]{0:T(256)S(1)} %slice.85), channel_id=1, source_target_pairs={{0,8},{8,16},{16,24},{24,32},{32,40},{40,48},{48,56},{56,64},{64,7... | collective-permute-start | bytes 2312 | tf_op jit(solution)/shard_map/ppermute | solution.py:59
  33.0 0.6 slice.81
  33.6 0.0 copy-done.5
  33.6 0.6 dynamic-slice
  34.9 0.0 copy-done
  34.9 0.1 multiply_reduce_fusion
  35.0 0.2 dynamic-update-slice
  35.2 14.8 %all-reduce.1 = f32[512]{0:T(512)S(1)} all-reduce(f32[512]{0:T(512)S(1)} %dynamic-update-slice), channel_id=4, replica_groups=mesh['genome'=32,'samples'=8] {'samples'}, use_global_device_ids=true, to_apply=%add.1 | all-reduce | flops 512 | bytes 4096
  50.0 0.1 reshape.63
  50.2 0.0 copy-done.3
  50.2 0.0 copy-done.4
  50.2 0.7 pad_bitcast_fusion
  50.9 0.0 collective-permute-done.1
  50.9 0.6 slice.77
  51.5 0.7 dynamic-slice_select_fusion.1
  52.2 0.1 pad_maximum_fusion
  52.3 0.0 all-gather.6.cloned.1.call-done
  52.3 3.7 %copy.24 = f32[8,8,8,1536]{3,2,1,0:T(8,128)S(1)} copy(f32[8,8,8,1536]{3,1,2,0:T(8,128)} %bitcast.45) | data formatting | bytes 6291456
  56.0 0.8 bitcast_reduce_fusion
  56.8 0.1 reduce_sum.50
  56.9 0.4 convolution_bitcast_fusion
  57.3 0.4 fusion.31
  57.8 0.2 copy_bitcast_fusion
  57.9 0.1 slice.79
  58.0 0.1 copy.22
  58.1 0.7 reshape.81
  58.8 10.8 %all-to-all-start = ((f32[32,1,128]{2,1,0:T(1,128)}), f32[32,1,128]{2,1,0:T(1,128)S(1)}, u32[]{:S(2)}, u32[]{:S(2)}) async-start(f32[32,1,128]{2,1,0:T(1,128)} %reshape.81), calls=%async_computation | async-start | bytes 32768 | tf_op jit(solution)/shard_map/all_to_all | solution.py:14
  69.7 0.2 fusion.9
  69.9 0.1 slice.83
  70.0 3.4 %collective-permute-start = (f32[192,64]{0,1:T(8,128)S(1)}, f32[192,64]{0,1:T(8,128)S(1)}, u32[]{:S(2)}, u32[]{:S(2)}) collective-permute-start(f32[192,64]{0,1:T(8,128)S(1)} %slice.83), channel_id=1, source_target_pairs={{0,8},{8,16},{16,24},{24,32},{32,40},{40,48},{48,56},{56,64},{64,7... | collective-permute-start | bytes 147464 | tf_op jit(solution)/shard_map/ppermute | solution.py:59
  73.4 4.2 %all-to-all-done = f32[32,1,128]{2,1,0:T(1,128)S(1)} async-done(((f32[32,1,128]{2,1,0:T(1,128)}), f32[32,1,128]{2,1,0:T(1,128)S(1)}, u32[]{:S(2)}, u32[]{:S(2)}) %all-to-all-start) | async-done | bytes 16416 | tf_op jit(solution)/shard_map/all_to_all | solution.py:14
  77.5 0.5 broadcast.51
  78.1 0.7 reduce.7
  78.7 0.1 reshape.82
  78.9 0.1 broadcast_select_fusion
  79.1 0.0 collective-permute-done
  79.1 0.2 slice_reduce_fusion
  79.3 0.7 add_multiply_fusion
  80.1 0.9 %fusion.8 = f32[16,64]{1,0:T(8,128)} fusion(f32[192,64]{0,1:T(8,128)S(1)} %get-tuple-element.5, f32[192,64]{0,1:T(8,128)S(1)} %get-tuple-element.6, s32[16]{0:T(128)S(1)} %get-tuple-element.9, s32[16]{0:T(128)S(1)} %get-tuple-element.10, f32[16]{0:T(128)S(1)} %fusion.9, f32[64]{0:T(128)S(1)} %multiply_add_fusion), kind=kOutput, calls=%fused_computation.10 | convolution fusion | flops 4776960 | bytes 102848 | tf_op jit(solution)/shard_map/dot_general | solution.py:141
  (24 shorter events, 0.4 us)
Async XLA Ops:
  7.2 45.1 %all-gather.6.cloned.1.call-start = ((), (), s32[]{:S(2)}) async-start(), calls=%async_computation.1 | async-start | bytes 3538944 | tf_op jit(solution)/shard_map/all_gather | solution.py:8
  11.5 16.9 %copy-start.1 = (s32[1536]{0:T(1024)S(1)}, s32[1536]{0:T(1024)}, u32[]{:S(2)}) copy-start(s32[1536]{0:T(1024)} %param.8) | copy-start | bytes 18436
  11.5 16.9 %copy-start.2 = (f32[8]{0:T(128)S(1)}, f32[8]{0:T(128)}, u32[]{:S(2)}) copy-start(f32[8]{0:T(128)} %param.9) | copy-start | bytes 100
  11.5 22.1 %copy-start.5 = (u32[256]{0:T(256)S(1)}, u32[256]{0:T(256)}, u32[]{:S(2)}) copy-start(u32[256]{0:T(256)} %constant.55) | copy-start | bytes 3076
  11.5 23.3 %copy-start = (bf16[1024,64]{0,1:T(8,128)(2,1)S(1)}, bf16[1024,64]{0,1:T(8,128)(2,1)}, u32[]{:S(2)}) copy-start(bf16[1024,64]{0,1:T(8,128)(2,1)} %param.7) | copy-start | bytes 393220
  11.6 38.6 %copy-start.3 = (s32[16]{0:T(128)S(1)}, s32[16]{0:T(128)}, u32[]{:S(2)}) copy-start(s32[16]{0:T(128)} %param.10) | copy-start | bytes 196
  11.6 38.6 %copy-start.4 = (s32[16]{0:T(128)S(1)}, s32[16]{0:T(128)}, u32[]{:S(2)}) copy-start(s32[16]{0:T(128)} %param.11) | copy-start | bytes 196
  29.2 21.7 %collective-permute-start.1 = (f32[192]{0:T(256)S(1)}, f32[192]{0:T(256)S(1)}, u32[]{:S(2)}, u32[]{:S(2)}) collective-permute-start(f32[192]{0:T(256)S(1)} %slice.85), channel_id=1, source_target_pairs={{0,8},{8,16},{16,24},{24,32},{32,40},{40,48},{48,56},{56,64},{64,7... | collective-permute-start | bytes 2312 | tf_op jit(solution)/shard_map/ppermute | solution.py:59
  58.8 18.7 %all-to-all-start = ((f32[32,1,128]{2,1,0:T(1,128)}), f32[32,1,128]{2,1,0:T(1,128)S(1)}, u32[]{:S(2)}, u32[]{:S(2)}) async-start(f32[32,1,128]{2,1,0:T(1,128)} %reshape.81), calls=%async_computation | async-start | bytes 32768 | tf_op jit(solution)/shard_map/all_to_all | solution.py:14
  70.0 9.2 %collective-permute-start = (f32[192,64]{0,1:T(8,128)S(1)}, f32[192,64]{0,1:T(8,128)S(1)}, u32[]{:S(2)}, u32[]{:S(2)}) collective-permute-start(f32[192,64]{0,1:T(8,128)S(1)} %slice.83), channel_id=1, source_target_pairs={{0,8},{8,16},{16,24},{24,32},{32,40},{40,48},{48,56},{56,64},{64,7... | collective-permute-start | bytes 147464 | tf_op jit(solution)/shard_map/ppermute | solution.py:59
Sparse Core Ops, SparseCore 0:
  11.6 33.2 all-gather.5
where the time goes:
time: 88.9 us; the launch traced here: 87.8 us
  blocking collectives  28.2 us (32%)
  starting transfers between devices  18.1 us (20%)
  between operations  15 us (17%)
  matrix products  9.39 us (11%)
  local copies, waits for them, and re-layouts  8.56 us (10%)
  other arithmetic  4.44 us (5%)
  waiting for transfers between devices  4.2 us (5%)
    unnamed x1, blocking collectives  14.8 us
    all_gather x1, blocking collectives, total_of_pieces(): blocks = lax.all_gather(x, axis)  13.3 us
    all_to_all x1, starting transfers between devices, from_everyone(): lax.all_to_all(jnp.broadcast_to(x[None], (peers, *x.shape)), axis, 0, 0,...  10.8 us
    ppermute x2, starting transfers between devices, passed_along(): lax.ppermute(value, axis, [(source, source + steps) for source in range(l...  7.21 us
    unnamed x18, local copies, waits for them, and re-layouts  5.33 us
    dot_general x1, matrix products, local(): lax.dot_general(dosage, residuals, contract, preferred_element_type=jnp.f...  4.27 us
    all_to_all x1, waiting for transfers between devices, from_everyone(): lax.all_to_all(jnp.broadcast_to(x[None], (peers, *x.shape)), axis, 0, 0,...  4.17 us
    dot_general x1, matrix products, local(): lax.dot_general(dosage * dosage, jnp.ones((sample_rows,), jnp.bfloat16),...  3.48 us
  transfers between devices with their start and end apart: 4, of which 1 were waited for; matrix products, arithmetic and copies ran while one was open for 11% of the time, Pallas kernels for 0%

commit v1 on v0

v1 whole, which is shorter than its diff:
```python
import functools
import jax
import jax.numpy as jnp
from jax import lax
from jax.experimental import pallas as pl
from jax.experimental.pallas import tpu as pltpu
from jax.sharding import PartitionSpec as P

MESH = pl.DeviceIdType.MESH
F32 = jnp.float32
BF16 = jnp.bfloat16
LANES = 128
HALF = 64
CHIP_STEPS = (2, 1, 3, 0)
NT = (((1,), (1,)), ((), ()))


def split3(x):
    hi = x.astype(BF16)
    rest = x - hi.astype(F32)
    mid = rest.astype(BF16)
    low = (rest - mid.astype(F32)).astype(BF16)
    return hi, mid, low


def select_rows(rows, x):
    total = None
    for part in split3(x):
        term = lax.dot_general(rows, part, NT, preferred_element_type=F32)
        total = term if total is None else total + term
    return total


def kernel(
    nx, nz, scale_score, scale_track, inv_samples,
    geno, resid, vclass, cweight, gstart, gend,
    track, gene,
    gbuf, rbuf, rt, cbuf, wbuf, cw_s, gs_s, ge_s,
    msg, inbox, tot, totbox, zsrc, zbox, xsrc, xbox, fsrc, fbox, lhs,
    load_sem, small_sem, rs_send, rs_recv, tot_send, tot_recv,
    z_send, z_recv, x_send, x_recv, f_send, f_recv,
):
    g = lax.axis_index("genome")
    s = lax.axis_index("samples")
    gx, gz = g // nz, g % nz
    y, c = s // 2, s % 2
    ng = nx * nz
    cols = 3 * LANES

    r_copy = pltpu.make_async_copy(resid, rbuf, small_sem.at[0])
    r_copy.start()
    small = [
        pltpu.make_async_copy(vclass, cbuf, small_sem.at[1]),
        pltpu.make_async_copy(cweight, cw_s, small_sem.at[2]),
        pltpu.make_async_copy(gstart, gs_s, small_sem.at[3]),
        pltpu.make_async_copy(gend, ge_s, small_sem.at[4]),
    ]
    for copy in small:
        copy.start()
    chips = [(y + step) % 4 for step in CHIP_STEPS]
    loads = []
    for k, chip in enumerate(chips):
        at = pl.multiple_of(chip * cols, LANES)
        loads.append(pltpu.make_async_copy(geno.at[:, pl.ds(at, cols)], gbuf.at[k], load_sem.at[k]))
        loads[-1].start()

    barrier = pltpu.get_barrier_semaphore()
    for d in range(1, 8):
        pl.semaphore_signal(barrier, inc=1, device_id=(g, (s + d) % 8), device_id_type=MESH)
    for d in range(1, nz):
        pl.semaphore_signal(barrier, inc=1, device_id=(gx * nz + (gz + d) % nz, s), device_id_type=MESH)
    for d in range(1, nx):
        pl.semaphore_signal(barrier, inc=1, device_id=(((gx + d) % nx) * nz + gz, s), device_id_type=MESH)

    @pl.when(s == 7)
    def _():
        pl.semaphore_signal(barrier, inc=1, device_id=((g + 1) % ng, 0), device_id_type=MESH)

    @pl.when(s == 0)
    def _():
        pl.semaphore_signal(barrier, inc=1, device_id=((g + ng - 1) % ng, 7), device_id_type=MESH)

    lane = lax.broadcasted_iota(jnp.int32, (8, LANES), 1)
    sub = lax.broadcasted_iota(jnp.int32, (8, LANES), 0)
    lane64 = lax.broadcasted_iota(jnp.int32, (64, LANES), 1)
    row64 = lax.broadcasted_iota(jnp.int32, (64, LANES), 0)
    low64 = lane64 < HALF
    low32 = low64[:32]
    diag = lane64 == row64

    r_copy.wait()
    resid_v = rbuf[...]
    eye = (lax.broadcasted_iota(jnp.int32, (64, 64), 0) == lax.broadcasted_iota(jnp.int32, (64, 64), 1)).astype(F32).astype(BF16)
    rt[...] = lax.dot_general(eye, resid_v, NT, preferred_element_type=F32).astype(BF16)
    resid_f = resid_v.astype(F32)
    spread_row = jnp.sum(resid_f * resid_f, axis=0, keepdims=True)
    spread_row = jnp.concatenate([spread_row, jnp.zeros((1, HALF), F32)], axis=1)

    for copy in small:
        copy.wait()
    cls = cbuf[...]
    weight = jnp.zeros(cls.shape, F32)
    for k in range(8):
        weight = jnp.where(cls == k, cw_s[k], weight)
    wbuf[...] = weight * scale_score

    base = (g * 8 + s) * 192
    lane16 = lax.broadcasted_iota(jnp.int32, (16, LANES), 1)
    row16 = lax.broadcasted_iota(jnp.int32, (16, LANES), 0)
    first = jnp.zeros((16, LANES), jnp.int32)
    last = jnp.zeros((16, LANES), jnp.int32)
    for k in range(16):
        first = jnp.where(row16 == k, gs_s[k] - base, first)
        last = jnp.where(row16 == k, ge_s[k] - 1 - base, last)
    tri_lane = lax.broadcasted_iota(jnp.int32, (192, LANES), 1)
    tri_row = lax.broadcasted_iota(jnp.int32, (192, LANES), 0)
    one = lambda m: m.astype(F32).astype(BF16)
    full_off, half_off = HALF * c, LANES * (1 - c)
    lhs[0:192, 0:LANES] = one(tri_lane + full_off <= tri_row)
    lhs[0:192, LANES:] = one((tri_lane + half_off <= tri_row) & (tri_lane < HALF))
    pos_f, pos_h = lane16 + full_off, lane16 + half_off
    pick_f = (pos_f >= first) & (pos_f <= last)
    pick_h = (pos_h >= first) & (pos_h <= last) & (lane16 < HALF)
    lhs[192:208, 0:LANES] = one(pick_f)
    lhs[192:208, LANES:] = one(pick_h)
    prior_f = lane16 + HALF * (1 - c) - 192 >= first
    prior_h = (lane16 + LANES * c - 192 >= first) & (lane16 < HALF)
    lhs[208:224, 0:LANES] = one(prior_f)
    lhs[208:224, LANES:] = one(prior_h)

    totals = jnp.zeros((8, LANES), F32)
    for k, chip in enumerate(chips):
        loads[k].wait()
        acc = jnp.zeros((64, cols), F32)
        square = jnp.zeros((8, cols), F32)
        for part in range(4):
            at = 256 * part
            dose = gbuf[k, at : at + 256, :].astype(F32)
            square = square + jnp.sum((dose * dose).reshape(32, 8, cols), axis=0)
            acc = acc + jnp.dot(rt[:, at : at + 256], dose.astype(BF16), preferred_element_type=F32)
        counts = jnp.sum(square, axis=0, keepdims=True)
        x, q = [], []
        for t in range(3):
            w = wbuf[pl.ds(3 * chip + t, 1), :]
            x.append(acc[:, t * LANES : (t + 1) * LANES] * w)
            q.append(counts[:, t * LANES : (t + 1) * LANES] * (w * w))
        turned = pltpu.roll(x[1], HALF, 1)
        halves = (
            jnp.where(low32, x[1][:32], turned[32:]),
            jnp.where(low32, turned[:32], x[1][32:]),
        )
        q_half = jnp.broadcast_to(q[1], (8, LANES))
        q_halves = (q_half, pltpu.roll(q_half, HALF, 1))
        for side in range(2):
            full = x[2 * side]
            msg[k, side, 0:64] = full
            msg[k, side, 64:96] = halves[side]
            msg[k, side, 96:104] = jnp.where(
                sub == 0, q[2 * side],
                jnp.where(sub == 1, q_halves[side], jnp.where(sub == 2, spread_row, 0.0)),
            )
            own_half = jnp.where(low64, x[1], 0.0) if side == 0 else jnp.where(low64, 0.0, x[1])
            column = jnp.sum(full + own_half, axis=1, keepdims=True)
            line = jnp.sum(jnp.where(diag, column, 0.0), axis=0, keepdims=True)
            totals = jnp.where(sub == 2 * chip + side, line, totals)
    tot[...] = totals

    pl.semaphore_wait(barrier, 7 + (nz - 1) + (nx - 1) + jnp.where((s == 0) | (s == 7), 1, 0))

    tot_copies = []
    for d in range(1, 8):
        tot_copies.append(pltpu.make_async_remote_copy(
            src_ref=tot, dst_ref=totbox.at[d - 1], send_sem=tot_send.at[d - 1], recv_sem=tot_recv.at[d - 1],
            device_id=(g, (s + d) % 8), device_id_type=MESH))
        tot_copies[-1].start()

    rs_copies = []
    for k in range(3):
        for side in range(2):
            slot = 2 * k + c
            rs_copies.append(pltpu.make_async_remote_copy(
                src_ref=msg.at[k, side], dst_ref=inbox.at[slot],
                send_sem=rs_send.at[2 * k + side], recv_sem=rs_recv.at[slot],
                device_id=(g, 2 * chips[k] + side), device_id_type=MESH))
            rs_copies[-1].start()
    rs_copies.append(pltpu.make_async_remote_copy(
        src_ref=msg.at[3, 1 - c], dst_ref=inbox.at[6], send_sem=rs_send.at[6], recv_sem=rs_recv.at[6],
        device_id=(g, 2 * y + 1 - c), device_id_type=MESH))
    rs_copies[-1].start()

    block_totals = totals
    for d in range(1, 8):
        tot_copies[d - 1].wait_recv()
        block_totals = block_totals + totbox[d - 1]
    group_total = jnp.sum(block_totals, axis=0, keepdims=True)
    carry = jnp.sum(jnp.where(sub < s, block_totals, 0.0), axis=0, keepdims=True)
    zsrc[...] = jnp.broadcast_to(group_total, (8, LANES))
    z_copies = []
    for d in range(1, nz):
        z_copies.append(pltpu.make_async_remote_copy(
            src_ref=zsrc, dst_ref=zbox.at[d - 1], send_sem=z_send.at[d - 1], recv_sem=z_recv.at[d - 1],
            device_id=(gx * nz + (gz + d) % nz, s), device_id_type=MESH))
        z_copies[-1].start()

    block = msg[3, c]
    for slot in range(7):
        pltpu.make_async_remote_copy(
            src_ref=msg.at[0, 0], dst_ref=inbox.at[slot], send_sem=rs_send.at[slot], recv_sem=rs_recv.at[slot],
            device_id=(g, s), device_id_type=MESH).wait_recv()
        block = block + inbox[slot]
    fsrc[...] = block
    following = s + 1
    f_copy = pltpu.make_async_remote_copy(
        src_ref=fsrc, dst_ref=fbox, send_sem=f_send, recv_sem=f_recv,
        device_id=((g + following // 8) % ng, following % 8), device_id_type=MESH)
    f_copy.start()

    def unpacked(packed):
        half = packed[64:96]
        wide = jnp.where(low64, jnp.concatenate([half, pltpu.roll(half, HALF, 1)], axis=0), 0.0)
        return jnp.concatenate([packed[0:64], wide], axis=1)

    local = select_rows(lhs[0:208], unpacked(block))
    prefix, score = local[0:192], local[192:208]
    zero = jnp.zeros((16, LANES), F32)
    quad = jnp.where(pick_f, block[96:97], zero) + jnp.where(pick_h, block[97:98], zero)

    line_total = group_total
    for d in range(1, nz):
        z_copies[d - 1].wait_recv()
        value = zbox[d - 1, 0:1]
        line_total = line_total + value
        carry = carry + jnp.where(gz >= d, value, 0.0)
    xsrc[...] = jnp.broadcast_to(line_total, (8, LANES))
    x_copies = []
    for d in range(1, nx):
        x_copies.append(pltpu.make_async_remote_copy(
            src_ref=xsrc, dst_ref=xbox.at[d - 1], send_sem=x_send.at[d - 1], recv_sem=x_recv.at[d - 1],
            device_id=(((gx + d) % nx) * nz + gz, s), device_id_type=MESH))
        x_copies[-1].start()

    f_copy.wait_recv()
    before = fbox[...]
    score = score + select_rows(lhs[208:224], unpacked(before))
    quad = quad + jnp.where(prior_f, before[96:97], zero) + jnp.where(prior_h, before[97:98], zero)
    quad = jnp.sum(quad, axis=1, keepdims=True)
    variance = block[98:99, 0:64] * inv_samples + 1e-5
    gene[...] = (score * score) / (variance * (quad + 1.0))

    for d in range(1, nx):
        x_copies[d - 1].wait_recv()
        carry = carry + jnp.where(gx >= d, xbox[d - 1, 0:1], 0.0)
    track[...] = prefix + carry[:, 0:64]

    for copy in tot_copies + rs_copies + z_copies + x_copies + [f_copy]:
        copy.wait_send()


def local(nx, nz, genotypes, residuals, variant_class, class_weight, gene_start, gene_end):
    rows, cols = genotypes.shape
    samples = rows * 8
    variants = cols * nx * nz
    anywhere = pl.BlockSpec(memory_space=pl.ANY)
    vmem = pl.BlockSpec(memory_space=pltpu.VMEM)
    dma = pltpu.SemaphoreType.DMA
    track, gene = pl.pallas_call(
        functools.partial(kernel, nx, nz, samples ** -0.5, variants ** -0.5, 1.0 / samples),
        out_shape=(jax.ShapeDtypeStruct((192, 64), F32), jax.ShapeDtypeStruct((16, 64), F32)),
        in_specs=[anywhere] * 6,
        out_specs=(vmem, vmem),
        scratch_shapes=[
            pltpu.VMEM((4, rows, 384), jnp.int32),
            pltpu.VMEM((rows, 64), BF16),
            pltpu.VMEM((64, rows), BF16),
            pltpu.VMEM((12, LANES), jnp.int32),
            pltpu.VMEM((12, LANES), F32),
            pltpu.SMEM((8,), F32),
            pltpu.SMEM((16,), jnp.int32),
            pltpu.SMEM((16,), jnp.int32),
            pltpu.VMEM((4, 2, 104, LANES), F32),
            pltpu.VMEM((7, 104, LANES), F32),
            pltpu.VMEM((8, LANES), F32),
            pltpu.VMEM((7, 8, LANES), F32),
            pltpu.VMEM((8, LANES), F32),
            pltpu.VMEM((nz - 1, 8, LANES), F32),
            pltpu.VMEM((8, LANES), F32),
            pltpu.VMEM((nx - 1, 8, LANES), F32),
            pltpu.VMEM((104, LANES), F32),
            pltpu.VMEM((104, LANES), F32),
            pltpu.VMEM((224, 256), BF16),
            dma((4,)), dma((5,)), dma((7,)), dma((7,)), dma((7,)), dma((7,)),
            dma((nz - 1,)), dma((nz - 1,)), dma((nx - 1,)), dma((nx - 1,)), dma, dma,
        ],
        compiler_params=pltpu.CompilerParams(collective_id=0, has_side_effects=True),
        name="burden",
    )(
        genotypes, residuals, variant_class.reshape(12, LANES), class_weight, gene_start, gene_end
    )
    return track * variants ** -0.5, gene


def solution(mesh):
    groups = mesh.shape["genome"]
    nz = 8 if groups % 8 == 0 else 2
    return jax.shard_map(
        functools.partial(local, groups // nz, nz),
        mesh=mesh,
        in_specs=(
            P("samples", "genome"),
            P("samples", None),
            P("genome"),
            P(),
            P(("genome", "samples")),
            P(("genome", "samples")),
        ),
        out_specs=(P(("genome", "samples"), None), P(("genome", "samples"), None)),
        check_vma=False,
    )
```

time: 88.9 us -> 29.5 us (0.33)
  the two profiles are of different devices: /device:TPU:6 before, /device:TPU:1 now
where the time goes in v1:
time: 29.5 us; the launch traced here: 29.3 us
  Pallas kernels  24 us (81%)
  local copies, waits for them, and re-layouts  3.74 us (13%)
  other arithmetic  0.9 us (3%)
  between operations  0.64 us (2%)
    pallas_call x1, Pallas kernels, local(): pl.pallas_call(functools.partial(kernel, nx, nz, samples ** (-0.5), varia...  24 us
    unnamed x3, local copies, waits for them, and re-layouts  3.74 us
    mul x1, other arithmetic, local(): return (track * variants ** (-0.5), gene)  0.9 us

profile of v1, /device:TPU:1, one launch (start us, length us, event | category | flops | bytes accessed | tf_op | source)
XLA Modules:
  0.0 29.3 jit_solution(7950110393596561822)
XLA Ops:
  0.6 1.7 %copy.8.resid = bf16[1024,64]{1,0:T(8,128)(2,1)} copy(bf16[1024,64]{0,1:T(8,128)(2,1)} %param.7) | data formatting | bytes 262144 | tf_op args[1]
  2.4 24.0 %burden.1 = (f32[192,64]{1,0:T(8,128)}, f32[16,64]{1,0:T(8,128)}) custom-call(s32[1024,1536]{1,0:T(8,128)} %geno.1, bf16[1024,64]{1,0:T(8,128)(2,1)} %copy.8.resid, s32[12,128]{1,0:T(8,128)} %bitcast.1, f32[8]{0:T(128)} %cweight.1, s32[16]{0:T(128)} %gstart.1, s32[16]{0:T(128)} %gend.1), custom_call_target="tpu_custom_call" | custom-call | tf_op jit(solution)/shard_map/burden/pallas_call | solution.py:266
  26.4 0.9 %broadcast_multiply_fusion = f32[192,64]{1,0:T(8,128)S(1)} fusion(f32[192,64]{1,0:T(8,128)} %get-tuple-element.4), kind=kLoop, calls=%fused_computation | loop fusion | flops 12288 | bytes 98304 | tf_op jit(solution)/shard_map/mul | solution.py:299
  27.3 0.7 %copy.9 = f32[192,64]{0,1:T(8,128)} copy(f32[192,64]{1,0:T(8,128)S(1)} %broadcast_multiply_fusion) | data formatting | bytes 98304
  28.0 1.3 %copy.11 = f32[16,64]{1,0:T(8,128)} copy(f32[16,64]{1,0:T(8,128)} %get-tuple-element.11) | data formatting | bytes 8192

commit v2 on v1

v2 whole, which is shorter than its diff:
```python
import functools
import jax
import jax.numpy as jnp
from jax import lax
from jax.experimental import pallas as pl
from jax.experimental.pallas import tpu as pltpu
from jax.sharding import PartitionSpec as P

MESH = pl.DeviceIdType.MESH
F32 = jnp.float32
BF16 = jnp.bfloat16
LANES = 128
HALF = 64
NT = (((1,), (1,)), ((), ()))


def split3(x):
    hi = x.astype(BF16)
    rest = x - hi.astype(F32)
    mid = rest.astype(BF16)
    low = (rest - mid.astype(F32)).astype(BF16)
    return hi, mid, low


def added_up(parts, multiply):
    total = None
    for part in parts:
        term = multiply(part)
        total = term if total is None else total + term
    return total


def dot_nt(a, b):
    return lax.dot_general(a, b, NT, preferred_element_type=F32)


CHIP_STEPS = (2, 1, 3, 0)


def is_low(group):
    return group % 8 < 4


def kernel(
    ng, scale_score, scale_track, inv_samples,
    geno, resid, vclass, cweight, gstart, gend,
    track, gene,
    gbuf, rt, cbuf, wbuf, cw_s, gs_s, ge_s,
    msg, pair_box, comb, inbox, gsum, gbox, cum, cbox, fsrc, fbox, lhs,
    load_sem, small_sem, pair_send, pair_recv, rs_send, rs_recv, g_send, g_recv, c_send, c_recv, f_send, n_send, f_recv,
    group_sem, far_sem,
):
    g = lax.axis_index("genome")
    s = lax.axis_index("samples")
    y, c = s // 2, s % 2
    nx, gx, gz = ng // 8, g // 8, g % 8
    cols = 3 * LANES

    def to_device(src, dst, send, recv, genome, sample):
        return pltpu.make_async_remote_copy(
            src_ref=src, dst_ref=dst, send_sem=send, recv_sem=recv,
            device_id=(genome, sample), device_id_type=MESH)

    r_copy = pltpu.make_async_copy(resid, rt, small_sem.at[0])
    r_copy.start()
    small = [
        pltpu.make_async_copy(vclass, cbuf, small_sem.at[1]),
        pltpu.make_async_copy(cweight, cw_s, small_sem.at[2]),
        pltpu.make_async_copy(gstart, gs_s, small_sem.at[3]),
        pltpu.make_async_copy(gend, ge_s, small_sem.at[4]),
    ]
    for copy in small:
        copy.start()
    chips = [(y + step) % 4 for step in CHIP_STEPS]
    rows_half = geno.shape[0] // 2
    loads = []
    for k in range(4):
        at = pl.multiple_of(chips[k] * cols, LANES)
        for h in range(2):
            rows = slice(h * rows_half, (h + 1) * rows_half)
            loads.append(pltpu.make_async_copy(
                geno.at[rows, pl.ds(at, cols)], gbuf.at[k, rows], load_sem.at[2 * k + h]))
    for copy in loads[:3]:
        copy.start()

    barrier = pltpu.get_barrier_semaphore()
    low = is_low(g)
    odd = c == 1
    last_group = g == ng - 1
    for d in range(1, 8):
        dest = (s + d) % 8

        @pl.when(dest % 2 == 1)
        def _():
            pl.semaphore_signal(barrier, inc=1, device_id=(g, dest), device_id_type=MESH)

    @pl.when((s == 0) & (g > 0))
    def _():
        for chip in range(4):
            pl.semaphore_signal(
                barrier, inc=1, device_id=(jnp.maximum(g - 1, 0), 2 * chip + 1), device_id_type=MESH)

    for copy in loads[3:]:
        copy.start()

    @pl.loop(0, g)
    def _(other):
        side = jnp.where(low & ~is_low(other), 1, 0)
        pl.semaphore_signal(barrier, inc=1, device_id=(other, 2 * y + side), device_id_type=MESH)

    later_low = (nx - 1 - gx) * 4 + jnp.where(low, 3 - gz, 0)
    later_high = (nx - 1 - gx) * 4 + jnp.where(low, 4, 7 - gz)
    group_count = 7 + jnp.where(last_group, 0, 1) + jnp.where(low, 0, 2 * later_low)
    far_count = 2 * (later_high + jnp.where(low, later_low, 0))

    lane = lax.broadcasted_iota(jnp.int32, (8, LANES), 1)
    sub = lax.broadcasted_iota(jnp.int32, (8, LANES), 0)
    lane64 = lax.broadcasted_iota(jnp.int32, (64, LANES), 1)
    row64 = lax.broadcasted_iota(jnp.int32, (64, LANES), 0)
    low64 = lane64 < HALF
    low32 = low64[:32]
    diag = lane64 == row64

    r_copy.wait()
    resid_f = rt[...].astype(F32)
    squares = resid_f * resid_f
    spread_col = squares[:, 0:LANES]
    for t in range(1, squares.shape[1] // LANES):
        spread_col = spread_col + squares[:, t * LANES : (t + 1) * LANES]
    spread_col = jnp.sum(spread_col, axis=1, keepdims=True)
    spread_row = jnp.sum(jnp.where(diag, spread_col, 0.0), axis=0, keepdims=True)

    for copy in small:
        copy.wait()
    cls = cbuf[...]
    weight = jnp.zeros(cls.shape, F32)
    for k in range(8):
        weight = jnp.where(cls == k, cw_s[k], weight)
    wbuf[...] = weight * scale_score

    base = (g * 8 + s) * 192
    lane16 = lax.broadcasted_iota(jnp.int32, (16, LANES), 1)
    row16 = lax.broadcasted_iota(jnp.int32, (16, LANES), 0)
    first = jnp.zeros((16, LANES), jnp.int32)
    last = jnp.zeros((16, LANES), jnp.int32)
    for k in range(16):
        first = jnp.where(row16 == k, gs_s[k] - base, first)
        last = jnp.where(row16 == k, ge_s[k] - 1 - base, last)
    tri_lane = lax.broadcasted_iota(jnp.int32, (192, LANES), 1)
    tri_row = lax.broadcasted_iota(jnp.int32, (192, LANES), 0)
    one = lambda m: m.astype(F32).astype(BF16)
    full_off, half_off = HALF * c, LANES * (1 - c)
    lhs[0:192, 0:LANES] = one(tri_lane + full_off <= tri_row)
    lhs[0:192, LANES:] = one((tri_lane + half_off <= tri_row) & (tri_lane < HALF))
    pos_f, pos_h = lane16 + full_off, lane16 + half_off
    pick_f = (pos_f >= first) & (pos_f <= last)
    pick_h = (pos_h >= first) & (pos_h <= last) & (lane16 < HALF)
    lhs[192:208, 0:LANES] = one(pick_f)
    lhs[192:208, LANES:] = one(pick_h)
    prior_f = lane16 + HALF * (1 - c) - 192 >= first
    prior_h = (lane16 + LANES * c - 192 >= first) & (lane16 < HALF)
    lhs[208:224, 0:LANES] = one(prior_f)
    lhs[208:224, LANES:] = one(prior_h)

    def product(k):
        acc = jnp.zeros((64, cols), F32)
        square = jnp.zeros((8, cols), F32)
        for part in range(4):
            if part % 2 == 0:
                loads[2 * k + part // 2].wait()
            at = 256 * part
            dose = gbuf[k, at : at + 256, :].astype(F32)
            square = square + jnp.sum((dose * dose).reshape(32, 8, cols), axis=0)
            acc = acc + jnp.dot(rt[:, at : at + 256], dose.astype(BF16), preferred_element_type=F32)
        return acc, jnp.sum(square, axis=0, keepdims=True)

    def packed_blocks(k, acc, counts):
        x, q, lines = [], [], []
        for t in range(3):
            w = wbuf[pl.ds(3 * chips[k] + t, 1), :]
            x.append(acc[:, t * LANES : (t + 1) * LANES] * w)
            q.append(counts[:, t * LANES : (t + 1) * LANES] * (w * w))
        turned = pltpu.roll(x[1], HALF, 1)
        halves = (
            jnp.where(low32, x[1][:32], turned[32:]),
            jnp.where(low32, turned[:32], x[1][32:]),
        )
        q_half = jnp.broadcast_to(q[1], (8, LANES))
        q_halves = (q_half, pltpu.roll(q_half, HALF, 1))
        for side in range(2):
            full = x[2 * side]
            msg[k, side, 0:64] = full
            msg[k, side, 64:96] = halves[side]
            msg[k, side, 96:104] = jnp.where(
                sub == 0, q[2 * side],
                jnp.where(sub == 1, q_halves[side], jnp.where(sub == 2, spread_row, 0.0)),
            )
            own_half = jnp.where(low64, x[1], 0.0) if side == 0 else jnp.where(low64, 0.0, x[1])
            column = jnp.sum(full + own_half, axis=1, keepdims=True)
            lines.append(jnp.sum(jnp.where(diag, column, 0.0), axis=0, keepdims=True))
        return lines

    def pair_copy(k):
        return to_device(msg.at[k, 1 - c], pair_box.at[k], pair_send, pair_recv.at[k], g, 2 * y + 1 - c)

    def group_is_here():
        @pl.when(odd)
        def _():
            pl.semaphore_wait(barrier, group_count)
            pl.semaphore_signal(group_sem, inc=1, device_id=(g, 2 * y), device_id_type=MESH)

        @pl.when(~odd)
        def _():
            pl.semaphore_wait(group_sem, 1)

    totals = jnp.zeros((8, LANES), F32)
    pending = None
    for k in range(5):
        result = product(k) if k < 4 else None
        if pending is not None:
            lines = packed_blocks(k - 1, *pending)
            for side in range(2):
                totals = jnp.where(sub == 2 * chips[k - 1] + side, lines[side], totals)
        if k == 2:
            group_is_here()
            pair_copy(0).start()
        if k >= 2:
            pair_copy(k - 1).start()
        pending = result
    running = jnp.zeros((1, LANES), F32)
    earlier = jnp.zeros((8, LANES), F32)
    for k in range(8):
        earlier = jnp.where(sub == k, running, earlier)
        running = running + totals[k : k + 1]
    gsum[...] = running

    def total_copy(later):
        ahead = later // 8 > gx
        send = jnp.where(ahead, later // 8, nx + later % 8)
        recv = jnp.where(ahead, gx, nx + gz)
        return to_device(gsum, gbox.at[g], g_send.at[send], g_recv.at[recv], later, s)

    @pl.loop(g + 1, ng)
    def _(later):
        @pl.when(~low & is_low(later))
        def _():
            total_copy(later).start()

    to_next = odd & ~last_group

    def next_copy(k):
        return to_device(comb.at[k], fbox.at[y], n_send, f_recv, jnp.minimum(g + 1, ng - 1), 0)

    for k in range(4):
        pair_copy(k).wait_recv()
        comb[k] = msg[k, c] + pair_box[k]
        if k < 3:
            to_device(comb.at[k], inbox.at[k], rs_send, rs_recv, g, 2 * chips[k] + c).start()

        @pl.when(to_next & (chips[k] == 3))
        def _():
            next_copy(k).start()

    @pl.when(~odd)
    def _():
        @pl.when(far_count > 0)
        def _():
            pl.semaphore_wait(barrier, far_count)

        pl.semaphore_signal(far_sem, inc=1, device_id=(g, 2 * y + 1), device_id_type=MESH)

    @pl.when(odd)
    def _():
        pl.semaphore_wait(far_sem, 1)

    @pl.loop(g + 1, ng)
    def _(later):
        @pl.when(low | ~is_low(later))
        def _():
            total_copy(later).start()

    inbox_copy = to_device(comb.at[0:3], inbox, rs_send, rs_recv, g, s ^ 1)
    inbox_copy.wait_recv()
    block = comb[3]
    for k in range(3):
        block = block + inbox[k]
    fsrc[...] = block
    f_copy = to_device(fsrc, fbox.at[0], f_send, f_recv, g, jnp.minimum(s + 1, 7))

    @pl.when(s != 7)
    def _():
        f_copy.start()

    def unpacked(packed):
        half = packed[64:96]
        wide = jnp.where(low64, jnp.concatenate([half, pltpu.roll(half, HALF, 1)], axis=0), 0.0)
        return jnp.concatenate([packed[0:64], wide], axis=1)

    parts = split3(unpacked(block))
    prefix = added_up(parts, lambda part: dot_nt(part, lhs[0:192]))
    score = added_up(parts, lambda part: dot_nt(lhs[192:208], part))
    zero = jnp.zeros((16, LANES), F32)
    quad = jnp.where(pick_f, block[96:97], zero) + jnp.where(pick_h, block[97:98], zero)

    def total_waits(wait, rows_wanted, places_wanted):
        for k in range(nx):
            @pl.when(rows_wanted(k))
            def _():
                row = gbox.at[8 * k : 8 * k + 8]
                wait(to_device(row, row, g_send.at[k], g_recv.at[k], g, s ^ 1))

        for k in range(8):
            @pl.when(places_wanted(k))
            def _():
                wait(to_device(gsum, gbox.at[k], g_send.at[nx + k], g_recv.at[nx + k], g, s ^ 1))

    total_waits(lambda copy: copy.wait_recv(), lambda k: k < gx, lambda k: k < gz)
    sums = [jnp.where(k < g, gbox[k], 0.0) for k in range(ng - 1)]
    while len(sums) > 1:
        sums = [sums[i] + sums[i + 1] if i + 1 < len(sums) else sums[i] for i in range(0, len(sums), 2)]
    earlier = earlier + sums[0]
    for k in range(8):
        cum[k] = earlier[k : k + 1]
    c_copies = []
    for d in range(1, 8):
        dest = (s + d) % 8
        c_copies.append(to_device(cum.at[dest], cbox.at[d - 1], c_send, c_recv, g, dest))
        c_copies[-1].start()

    @pl.when(s != 0)
    def _():
        f_copy.wait_recv()

    @pl.when((s == 0) & (g > 0))
    def _():
        to_device(fbox, fbox, f_send, f_recv, g, s ^ 1).wait_recv()

    before = jnp.where((s != 0) | (g > 0), fbox[0], 0.0)
    for k in range(1, 4):
        before = before + jnp.where((s == 0) & (g > 0), fbox[k], 0.0)
    score = score + added_up(split3(unpacked(before)), lambda part: dot_nt(lhs[208:224], part))
    quad = quad + jnp.where(prior_f, before[96:97], zero) + jnp.where(prior_h, before[97:98], zero)
    quad = jnp.sum(quad, axis=1, keepdims=True)
    variance = block[98:99, 0:64] * inv_samples + 1e-5
    gene[...] = (score * score) / (variance * (quad + 1.0))

    to_device(cbox, cbox, c_send, c_recv, g, s ^ 1).wait_recv()
    carry = cum[s]
    for d in range(1, 8):
        carry = carry + cbox[d - 1]
    carry_col = jnp.sum(jnp.where(diag, carry, 0.0), axis=1, keepdims=True)
    track[...] = (prefix + carry_col) * scale_track

    to_device(cbox, cbox, c_send, c_recv, g, s ^ 1).wait_send()
    inbox_copy.wait_send()
    to_device(pair_box, pair_box, pair_send, rs_recv, g, s ^ 1).wait_send()

    @pl.when(s != 7)
    def _():
        f_copy.wait_send()

    @pl.when(to_next)
    def _():
        next_copy(0).wait_send()

    total_waits(lambda copy: copy.wait_send(), lambda k: k > gx, lambda k: k > gz)


def finish(track_in, gene_in, track, gene):
    track[...] = track_in[...]
    gene[...] = gene_in[...]


def finished(track, gene):
    vmem = pl.BlockSpec(memory_space=pltpu.VMEM)
    track, gene = pl.pallas_call(
        finish,
        out_shape=(jax.ShapeDtypeStruct(track.shape, F32), jax.ShapeDtypeStruct(gene.shape, F32)),
        in_specs=[vmem, vmem],
        out_specs=(vmem, vmem),
        compiler_params=pltpu.CompilerParams(vmem_limit_bytes=1 << 20),
        name="finish",
    )(track, gene)
    return track.T, gene


def local(ng, genotypes, residuals, variant_class, class_weight, gene_start, gene_end):
    rows, cols = genotypes.shape
    samples = rows * 8
    variants = cols * ng
    anywhere = pl.BlockSpec(memory_space=pl.ANY)
    vmem = pl.BlockSpec(memory_space=pltpu.VMEM)
    dma = pltpu.SemaphoreType.DMA
    track, gene = pl.pallas_call(
        functools.partial(kernel, ng, samples ** -0.5, variants ** -0.5, 1.0 / samples),
        out_shape=(pltpu.VMEM((64, 192), F32), pltpu.VMEM((16, 64), F32)),
        in_specs=[anywhere] * 6,
        out_specs=(vmem, vmem),
        scratch_shapes=[
            pltpu.VMEM((4, rows, 384), jnp.int32),
            pltpu.VMEM((64, rows), BF16),
            pltpu.VMEM((12, LANES), jnp.int32),
            pltpu.VMEM((12, LANES), F32),
            pltpu.SMEM((8,), F32),
            pltpu.SMEM((16,), jnp.int32),
            pltpu.SMEM((16,), jnp.int32),
            pltpu.VMEM((4, 2, 104, LANES), F32),
            pltpu.VMEM((4, 104, LANES), F32),
            pltpu.VMEM((4, 104, LANES), F32),
            pltpu.VMEM((3, 104, LANES), F32),
            pltpu.VMEM((1, LANES), F32),
            pltpu.VMEM((ng, 1, LANES), F32),
            pltpu.VMEM((8, 1, LANES), F32),
            pltpu.VMEM((7, 1, LANES), F32),
            pltpu.VMEM((104, LANES), F32),
            pltpu.VMEM((4, 104, LANES), F32),
            pltpu.VMEM((224, 256), BF16),
            dma((8,)), dma((5,)), dma, dma((4,)), dma, dma, dma((ng // 8 + 8,)), dma((ng // 8 + 8,)), dma, dma, dma, dma, dma,
            pltpu.SemaphoreType.REGULAR, pltpu.SemaphoreType.REGULAR,
        ],
        compiler_params=pltpu.CompilerParams(collective_id=0, has_side_effects=True),
        name="burden",
    )(
        genotypes, residuals.T, variant_class.reshape(12, LANES), class_weight, gene_start, gene_end
    )
    return finished(track, gene)


def solution(mesh):
    return jax.shard_map(
        functools.partial(local, mesh.shape["genome"]),
        mesh=mesh,
        in_specs=(
            P("samples", "genome"),
            P("samples", None),
            P("genome"),
            P(),
            P(("genome", "samples")),
            P(("genome", "samples")),
        ),
        out_specs=(P(("genome", "samples"), None), P(("genome", "samples"), None)),
        check_vma=False,
    )
```

time: 29.5 us -> 20.3 us (0.69)
  the two profiles are of different devices: /device:TPU:1 before, /device:TPU:6 now
where the time goes in v2:
time: 20.3 us
  Pallas kernels  19.6 us (97%)
  between operations  0.64 us (3%)
    pallas_call x1, Pallas kernels, local(): pl.pallas_call(functools.partial(kernel, ng, samples ** (-0.5), variants...  19 us
    pallas_call x1, Pallas kernels, finished(): pl.pallas_call(finish, out_shape=(jax.ShapeDtypeStruct(track.shape, F32),...  0.64 us

profile of v2, /device:TPU:6, one launch (start us, length us, event | category | flops | bytes accessed | tf_op | source)
XLA Modules:
  0.0 20.3 jit_solution(1464710464670100194)
XLA Ops:
  0.6 19.0 %burden.1 = (f32[64,192]{1,0:T(8,128)S(1)}, f32[16,64]{1,0:T(8,128)S(1)}) custom-call(s32[1024,1536]{1,0:T(8,128)} %geno.1, bf16[64,1024]{1,0:T(8,128)(2,1)} %bitcast.3, s32[12,128]{1,0:T(8,128)} %bitcast.4, f32[8]{0:T(128)} %cweight.1, s32[16]{0:T(128)} %gstart.1, s32[16]{0:T(128)} %gend.1), custom_call_target="tpu_custom_call" | custom-call | tf_op jit(solution)/shard_map/burden/pallas_call | solution.py:394
  19.6 0.6 %finish.1 = (f32[64,192]{1,0:T(8,128)}, f32[16,64]{1,0:T(8,128)}) custom-call(f32[64,192]{1,0:T(8,128)S(1)} %get-tuple-element.6.track_in, f32[16,64]{1,0:T(8,128)S(1)} %get-tuple-element.7.gene_in), custom_call_target="tpu_custom_call" | custom-call | tf_op jit(solution)/shard_map/finish/pallas_call | solution.py:376

commit v3 on v2

--- a/solution.py
+++ b/solution.py
@@ -30,6 +30,13 @@
     return total
 
 
+def tree_sum(terms):
+    while len(terms) > 1:
+        pairs = [terms[i] + terms[i + 1] for i in range(0, len(terms) - 1, 2)]
+        terms = pairs + terms[len(terms) - len(terms) % 2 :]
+    return terms[0]
+
+
 def dot_nt(a, b):
     return lax.dot_general(a, b, NT, preferred_element_type=F32)
 
@@ -46,9 +53,9 @@
     geno, resid, vclass, cweight, gstart, gend,
     track, gene,
     gbuf, rt, cbuf, wbuf, cw_s, gs_s, ge_s,
-    msg, pair_box, comb, inbox, gsum, gbox, cum, cbox, fsrc, fbox, lhs,
-    load_sem, small_sem, pair_send, pair_recv, rs_send, rs_recv, g_send, g_recv, c_send, c_recv, f_send, n_send, f_recv,
-    group_sem, far_sem,
+    msg, pair_box, comb, inbox, gsum, gtot, gbox, dbox, cum, cbox, fsrc, fbox, lhs,
+    load_sem, small_sem, pair_send, pair_recv, rs_send, rs_recv, g_send, g_recv, d_send, d_recv, c_send, c_recv, f_send, n_send, f_recv,
+    group_sem, far_sem, late_sem,
 ):
     g = lax.axis_index("genome")
     s = lax.axis_index("samples")
@@ -103,15 +110,40 @@
     for copy in loads[3:]:
         copy.start()
 
-    @pl.loop(0, g)
-    def _(other):
-        side = jnp.where(low & ~is_low(other), 1, 0)
-        pl.semaphore_signal(barrier, inc=1, device_id=(other, 2 * y + side), device_id_type=MESH)
-
-    later_low = (nx - 1 - gx) * 4 + jnp.where(low, 3 - gz, 0)
+    def tell(group, chip_list):
+        for chip in chip_list:
+            pl.semaphore_signal(barrier, inc=1, device_id=(group, 2 * chip), device_id_type=MESH)
+
+    @pl.when(low)
+    def _():
+        @pl.loop(0, gx)
+        def _(row):
+            for place in range(7, -1, -1):
+                tell(8 * row + place, range(4))
+
+        @pl.loop(0, gz)
+        def _(place):
+            tell(8 * gx + place, [y])
+
+        @pl.loop(gx, nx)
+        def _(row):
+            for place in range(4, 8):
+                tell(8 * row + place, [y])
+
+    @pl.when(~low)
+    def _():
+        @pl.loop(gz + 1, 8)
+        def _(place):
+            tell(8 * gx + place, [y])
+
+        @pl.loop(gx + 1, nx)
+        def _(row):
+            for place in range(4, 8):
+                tell(8 * row + place, [y])
+
     later_high = (nx - 1 - gx) * 4 + jnp.where(low, 4, 7 - gz)
-    group_count = 7 + jnp.where(last_group, 0, 1) + jnp.where(low, 0, 2 * later_low)
-    far_count = 2 * (later_high + jnp.where(low, later_low, 0))
+    group_count = 7 + jnp.where(last_group, 0, 1)
+    far_count = 32 * (nx - 1 - gx) + 2 * jnp.where(low, 3 - gz, 4 * (gx + 1) + 4 * gx + gz - 4)
 
     lane = lax.broadcasted_iota(jnp.int32, (8, LANES), 1)
     sub = lax.broadcasted_iota(jnp.int32, (8, LANES), 0)
@@ -228,23 +260,52 @@
             pair_copy(k - 1).start()
         pending = result
     running = jnp.zeros((1, LANES), F32)
-    earlier = jnp.zeros((8, LANES), F32)
     for k in range(8):
-        earlier = jnp.where(sub == k, running, earlier)
+        cum[k, 1] = running
         running = running + totals[k : k + 1]
     gsum[...] = running
+    for k in range(8):
+        cum[k, 0] = running
+
+    for d in range(1, 8):
+        dest = (s + d) % 8
+        to_device(cum.at[dest], cbox.at[d - 1], c_send, c_recv, g, dest).start()
 
     def total_copy(later):
         ahead = later // 8 > gx
         send = jnp.where(ahead, later // 8, nx + later % 8)
         recv = jnp.where(ahead, gx, nx + gz)
-        return to_device(gsum, gbox.at[g], g_send.at[send], g_recv.at[recv], later, s)
-
-    @pl.loop(g + 1, ng)
-    def _(later):
-        @pl.when(~low & is_low(later))
-        def _():
-            total_copy(later).start()
+        return to_device(gtot, gbox.at[g], g_send.at[send], g_recv.at[recv], later, s)
+
+    def chip_knows_groups():
+        @pl.when(~odd)
+        def _():
+            @pl.when(far_count > 0)
+            def _():
+                pl.semaphore_wait(barrier, far_count)
+
+            pl.semaphore_signal(far_sem, inc=1, device_id=(g, 2 * y + 1), device_id_type=MESH)
+
+        @pl.when(odd)
+        def _():
+            pl.semaphore_wait(far_sem, 1)
+
+    def direct_sends(place):
+        @pl.loop(gx + 1, nx)
+        def _(row):
+            for d in range(8):
+                slot = 64 * gx + 8 * gz + s
+                to_device(gsum, dbox.at[slot], d_send.at[row], d_recv.at[gx], 8 * row + place, d).start()
+
+    @pl.when(~low)
+    def _():
+        chip_knows_groups()
+
+        @pl.loop(0, g)
+        def _(other):
+            pl.semaphore_signal(late_sem, inc=1, device_id=(other, s), device_id_type=MESH)
+
+        direct_sends(0)
 
     to_next = odd & ~last_group
 
@@ -261,23 +322,43 @@
         def _():
             next_copy(k).start()
 
-    @pl.when(~odd)
-    def _():
-        @pl.when(far_count > 0)
-        def _():
-            pl.semaphore_wait(barrier, far_count)
-
-        pl.semaphore_signal(far_sem, inc=1, device_id=(g, 2 * y + 1), device_id_type=MESH)
-
-    @pl.when(odd)
-    def _():
-        pl.semaphore_wait(far_sem, 1)
-
-    @pl.loop(g + 1, ng)
-    def _(later):
-        @pl.when(low | ~is_low(later))
-        def _():
-            total_copy(later).start()
+    @pl.when(low)
+    def _():
+        chip_knows_groups()
+        direct_sends(0)
+
+    @pl.loop(1, 4)
+    def _(place):
+        direct_sends(place)
+
+    to_device(cbox, cbox, c_send, c_recv, g, s ^ 1).wait_recv()
+    group_total = running
+    carry = cum[s, 1]
+    for d in range(1, 8):
+        group_total = group_total + cbox[d - 1, 0]
+        carry = carry + cbox[d - 1, 1]
+    gtot[...] = group_total
+
+    @pl.when(low)
+    def _():
+        @pl.loop(gz + 1, 4)
+        def _(place):
+            total_copy(8 * gx + place).start()
+
+    def sends_to_late():
+        @pl.when(later_high > 0)
+        def _():
+            pl.semaphore_wait(late_sem, later_high)
+
+            @pl.loop(g + 1, ng)
+            def _(later):
+                @pl.when(~is_low(later))
+                def _():
+                    total_copy(later).start()
+
+    @pl.when(~low)
+    def _():
+        sends_to_late()
 
     inbox_copy = to_device(comb.at[0:3], inbox, rs_send, rs_recv, g, s ^ 1)
     inbox_copy.wait_recv()
@@ -302,30 +383,25 @@
     zero = jnp.zeros((16, LANES), F32)
     quad = jnp.where(pick_f, block[96:97], zero) + jnp.where(pick_h, block[97:98], zero)
 
-    def total_waits(wait, rows_wanted, places_wanted):
+    @pl.when(low)
+    def _():
+        sends_to_late()
+
+    def total_waits(wait, count, row_wanted, place_wanted):
         for k in range(nx):
-            @pl.when(rows_wanted(k))
+            @pl.when(row_wanted(k))
             def _():
-                row = gbox.at[8 * k : 8 * k + 8]
-                wait(to_device(row, row, g_send.at[k], g_recv.at[k], g, s ^ 1))
+                box = gbox.at[8 * k : 8 * k + count]
+                wait(to_device(box, box, g_send.at[k], g_recv.at[k], g, s ^ 1))
 
         for k in range(8):
-            @pl.when(places_wanted(k))
+            @pl.when(place_wanted(k))
             def _():
-                wait(to_device(gsum, gbox.at[k], g_send.at[nx + k], g_recv.at[nx + k], g, s ^ 1))
-
-    total_waits(lambda copy: copy.wait_recv(), lambda k: k < gx, lambda k: k < gz)
-    sums = [jnp.where(k < g, gbox[k], 0.0) for k in range(ng - 1)]
-    while len(sums) > 1:
-        sums = [sums[i] + sums[i + 1] if i + 1 < len(sums) else sums[i] for i in range(0, len(sums), 2)]
-    earlier = earlier + sums[0]
-    for k in range(8):
-        cum[k] = earlier[k : k + 1]
-    c_copies = []
-    for d in range(1, 8):
-        dest = (s + d) % 8
-        c_copies.append(to_device(cum.at[dest], cbox.at[d - 1], c_send, c_recv, g, dest))
-        c_copies[-1].start()
+                wait(to_device(gtot, gbox.at[k], g_send.at[nx + k], g_recv.at[nx + k], g, s ^ 1))
+
+    total_waits(lambda copy: copy.wait_recv(), 8, lambda k: ~low & (k < gx), lambda k: k < gz)
+    sums = [jnp.where((k < g) & (~low | (k // 8 == gx)), gbox[k], 0.0) for k in range(ng - 1)]
+    carry = carry + tree_sum(sums)
 
     @pl.when(s != 0)
     def _():
@@ -344,10 +420,15 @@
     variance = block[98:99, 0:64] * inv_samples + 1e-5
     gene[...] = (score * score) / (variance * (quad + 1.0))
 
-    to_device(cbox, cbox, c_send, c_recv, g, s ^ 1).wait_recv()
-    carry = cum[s]
-    for d in range(1, 8):
-        carry = carry + cbox[d - 1]
+    for k in range(nx - 1):
+        @pl.when(low & (k < gx))
+        def _():
+            row = dbox.at[64 * k : 64 * k + 64]
+            to_device(row, row, d_send.at[0], d_recv.at[k], g, s ^ 1).wait_recv()
+
+    direct = [tree_sum([dbox[64 * k + j] for j in range(64)]) for k in range(nx - 1)]
+    for k in range(nx - 1):
+        carry = carry + jnp.where(low & (k < gx), direct[k], 0.0)
     carry_col = jnp.sum(jnp.where(diag, carry, 0.0), axis=1, keepdims=True)
     track[...] = (prefix + carry_col) * scale_track
 
@@ -363,7 +444,11 @@
     def _():
         next_copy(0).wait_send()
 
-    total_waits(lambda copy: copy.wait_send(), lambda k: k > gx, lambda k: k > gz)
+    total_waits(lambda copy: copy.wait_send(), 4, lambda k: k > gx, lambda k: k > gz)
+    for k in range(1, nx):
+        @pl.when(k > gx)
+        def _():
+            to_device(dbox.at[0:32], dbox.at[0:32], d_send.at[k], d_recv.at[0], g, s ^ 1).wait_send()
 
 
 def finish(track_in, gene_in, track, gene):
@@ -409,14 +494,16 @@
             pltpu.VMEM((4, 104, LANES), F32),
             pltpu.VMEM((3, 104, LANES), F32),
             pltpu.VMEM((1, LANES), F32),
+            pltpu.VMEM((1, LANES), F32),
             pltpu.VMEM((ng, 1, LANES), F32),
-            pltpu.VMEM((8, 1, LANES), F32),
-            pltpu.VMEM((7, 1, LANES), F32),
+            pltpu.VMEM((8 * ng - 64, 1, LANES), F32),
+            pltpu.VMEM((8, 2, 1, LANES), F32),
+            pltpu.VMEM((7, 2, 1, LANES), F32),
             pltpu.VMEM((104, LANES), F32),
             pltpu.VMEM((4, 104, LANES), F32),
             pltpu.VMEM((224, 256), BF16),
-            dma((8,)), dma((5,)), dma, dma((4,)), dma, dma, dma((ng // 8 + 8,)), dma((ng // 8 + 8,)), dma, dma, dma, dma, dma,
-            pltpu.SemaphoreType.REGULAR, pltpu.SemaphoreType.REGULAR,
+            dma((8,)), dma((5,)), dma, dma((4,)), dma, dma, dma((ng // 8 + 8,)), dma((ng // 8 + 8,)), dma((ng // 8,)), dma((ng // 8,)), dma, dma, dma, dma, dma,
+            pltpu.SemaphoreType.REGULAR, pltpu.SemaphoreType.REGULAR, pltpu.SemaphoreType.REGULAR,
         ],
         compiler_params=pltpu.CompilerParams(collective_id=0, has_side_effects=True),
         name="burden",

time: 20.3 us -> 19.5 us (0.961)
  the two profiles are of different devices: /device:TPU:6 before, /device:TPU:2 now
where the time goes in v3:
time: 19.5 us
  Pallas kernels  18.8 us (96%)
  between operations  0.64 us (3%)
    pallas_call x1, Pallas kernels, local(): pl.pallas_call(functools.partial(kernel, ng, samples ** (-0.5), variants...  18.2 us
    pallas_call x1, Pallas kernels, finished(): pl.pallas_call(finish, out_shape=(jax.ShapeDtypeStruct(track.shape, F32),...  0.64 us

profile of v3, /device:TPU:2, one launch (start us, length us, event | category | flops | bytes accessed | tf_op | source)
XLA Modules:
  0.0 19.5 jit_solution(11205286730019997409)
XLA Ops:
  0.6 18.2 %burden.1 = (f32[64,192]{1,0:T(8,128)S(1)}, f32[16,64]{1,0:T(8,128)S(1)}) custom-call(s32[1024,1536]{1,0:T(8,128)} %geno.1, bf16[64,1024]{1,0:T(8,128)(2,1)} %bitcast.3, s32[12,128]{1,0:T(8,128)} %bitcast.4, f32[8]{0:T(128)} %cweight.1, s32[16]{0:T(128)} %gstart.1, s32[16]{0:T(128)} %gend.1), custom_call_target="tpu_custom_call" | custom-call | tf_op jit(solution)/shard_map/burden/pallas_call | solution.py:479
  18.8 0.6 %finish.1 = (f32[64,192]{1,0:T(8,128)}, f32[16,64]{1,0:T(8,128)}) custom-call(f32[64,192]{1,0:T(8,128)S(1)} %get-tuple-element.6.track_in, f32[16,64]{1,0:T(8,128)S(1)} %get-tuple-element.7.gene_in), custom_call_target="tpu_custom_call" | custom-call | tf_op jit(solution)/shard_map/finish/pallas_call | solution.py:461

commit v4 on v3

--- a/solution.py
+++ b/solution.py
@@ -297,15 +297,24 @@
                 slot = 64 * gx + 8 * gz + s
                 to_device(gsum, dbox.at[slot], d_send.at[row], d_recv.at[gx], 8 * row + place, d).start()
 
-    @pl.when(~low)
-    def _():
+    def all_direct_sends():
         chip_knows_groups()
 
-        @pl.loop(0, g)
-        def _(other):
-            pl.semaphore_signal(late_sem, inc=1, device_id=(other, s), device_id_type=MESH)
-
-        direct_sends(0)
+        @pl.when(~low)
+        def _():
+            @pl.loop(0, g)
+            def _(other):
+                pl.semaphore_signal(late_sem, inc=1, device_id=(other, s), device_id_type=MESH)
+
+        @pl.loop(0, 4)
+        def _(place):
+            direct_sends(place)
+
+    sends_first = ~low & (gx >= nx // 2)
+
+    @pl.when(sends_first)
+    def _():
+        all_direct_sends()
 
     to_next = odd & ~last_group
 
@@ -322,14 +331,9 @@
         def _():
             next_copy(k).start()
 
-    @pl.when(low)
-    def _():
-        chip_knows_groups()
-        direct_sends(0)
-
-    @pl.loop(1, 4)
-    def _(place):
-        direct_sends(place)
+    @pl.when(~sends_first)
+    def _():
+        all_direct_sends()
 
     to_device(cbox, cbox, c_send, c_recv, g, s ^ 1).wait_recv()
     group_total = running

time: 19.5 us -> 18.8 us (0.964)
  the two profiles are of different devices: /device:TPU:2 before, /device:TPU:6 now
where the time goes in v4:
time: 18.8 us; the launch traced here: 18.7 us
  Pallas kernels  18 us (96%)
  between operations  0.64 us (3%)
    pallas_call x1, Pallas kernels, local(): pl.pallas_call(functools.partial(kernel, ng, samples ** (-0.5), variants...  17.4 us
    pallas_call x1, Pallas kernels, finished(): pl.pallas_call(finish, out_shape=(jax.ShapeDtypeStruct(track.shape, F32),...  0.64 us

profile of v4, /device:TPU:6, one launch (start us, length us, event | category | flops | bytes accessed | tf_op | source)
XLA Modules:
  0.0 18.7 jit_solution(11185105420752933373)
XLA Ops:
  0.6 17.4 %burden.1 = (f32[64,192]{1,0:T(8,128)S(1)}, f32[16,64]{1,0:T(8,128)S(1)}) custom-call(s32[1024,1536]{1,0:T(8,128)} %geno.1, bf16[64,1024]{1,0:T(8,128)(2,1)} %bitcast.3, s32[12,128]{1,0:T(8,128)} %bitcast.4, f32[8]{0:T(128)} %cweight.1, s32[16]{0:T(128)} %gstart.1, s32[16]{0:T(128)} %gend.1), custom_call_target="tpu_custom_call" | custom-call | tf_op jit(solution)/shard_map/burden/pallas_call | solution.py:483
  18.0 0.6 %finish.1 = (f32[64,192]{1,0:T(8,128)}, f32[16,64]{1,0:T(8,128)}) custom-call(f32[64,192]{1,0:T(8,128)S(1)} %get-tuple-element.6.track_in, f32[16,64]{1,0:T(8,128)S(1)} %get-tuple-element.7.gene_in), custom_call_target="tpu_custom_call" | custom-call | tf_op jit(solution)/shard_map/finish/pallas_call | solution.py:465

commit v5 on v4

--- a/solution.py
+++ b/solution.py
@@ -196,14 +196,16 @@
 
     def product(k):
         acc = jnp.zeros((64, cols), F32)
-        square = jnp.zeros((8, cols), F32)
+        square = jnp.zeros((16, cols), F32)
         for part in range(4):
             if part % 2 == 0:
                 loads[2 * k + part // 2].wait()
             at = 256 * part
             dose = gbuf[k, at : at + 256, :].astype(F32)
-            square = square + jnp.sum((dose * dose).reshape(32, 8, cols), axis=0)
-            acc = acc + jnp.dot(rt[:, at : at + 256], dose.astype(BF16), preferred_element_type=F32)
+            dose = dose.astype(BF16)
+            squares = dose * dose
+            square = square + tree_sum([squares[i : i + 16] for i in range(0, 256, 16)]).astype(F32)
+            acc = acc + jnp.dot(rt[:, at : at + 256], dose, preferred_element_type=F32)
         return acc, jnp.sum(square, axis=0, keepdims=True)
 
     def packed_blocks(k, acc, counts):
@@ -272,10 +274,19 @@
         to_device(cum.at[dest], cbox.at[d - 1], c_send, c_recv, g, dest).start()
 
     def total_copy(later):
-        ahead = later // 8 > gx
-        send = jnp.where(ahead, later // 8, nx + later % 8)
-        recv = jnp.where(ahead, gx, nx + gz)
-        return to_device(gtot, gbox.at[g], g_send.at[send], g_recv.at[recv], later, s)
+        return to_device(gtot, gbox.at[g], g_send, g_recv, later, s)
+
+    def wait_for(wait, box, send, recv, number, choices):
+        for k in choices:
+            @pl.when(number == k)
+            def _():
+                wait(to_device(box(k), box(k), send, recv, g, s ^ 1))
+
+    def received(copy):
+        copy.wait_recv()
+
+    def sent(copy):
+        copy.wait_send()
 
     def chip_knows_groups():
         @pl.when(~odd)
@@ -295,7 +306,7 @@
         def _(row):
             for d in range(8):
                 slot = 64 * gx + 8 * gz + s
-                to_device(gsum, dbox.at[slot], d_send.at[row], d_recv.at[gx], 8 * row + place, d).start()
+                to_device(gsum, dbox.at[slot], d_send, d_recv, 8 * row + place, d).start()
 
     def all_direct_sends():
         chip_knows_groups()
@@ -391,19 +402,10 @@
     def _():
         sends_to_late()
 
-    def total_waits(wait, count, row_wanted, place_wanted):
-        for k in range(nx):
-            @pl.when(row_wanted(k))
-            def _():
-                box = gbox.at[8 * k : 8 * k + count]
-                wait(to_device(box, box, g_send.at[k], g_recv.at[k], g, s ^ 1))
-
-        for k in range(8):
-            @pl.when(place_wanted(k))
-            def _():
-                wait(to_device(gtot, gbox.at[k], g_send.at[nx + k], g_recv.at[nx + k], g, s ^ 1))
-
-    total_waits(lambda copy: copy.wait_recv(), 8, lambda k: ~low & (k < gx), lambda k: k < gz)
+    late_places = [k for k in range(ng) if not is_low(k)]
+    wait_for(received, lambda k: gbox.at[0:k], g_send, g_recv, jnp.where(low, 0, g), late_places)
+    wait_for(
+        received, lambda k: gbox.at[pl.ds(8 * gx, k)], g_send, g_recv, jnp.where(low, gz, 0), range(1, 4))
     sums = [jnp.where((k < g) & (~low | (k // 8 == gx)), gbox[k], 0.0) for k in range(ng - 1)]
     carry = carry + tree_sum(sums)
 
@@ -424,12 +426,7 @@
     variance = block[98:99, 0:64] * inv_samples + 1e-5
     gene[...] = (score * score) / (variance * (quad + 1.0))
 
-    for k in range(nx - 1):
-        @pl.when(low & (k < gx))
-        def _():
-            row = dbox.at[64 * k : 64 * k + 64]
-            to_device(row, row, d_send.at[0], d_recv.at[k], g, s ^ 1).wait_recv()
-
+    wait_for(received, lambda k: dbox.at[0 : 64 * k], d_send, d_recv, jnp.where(low, gx, 0), range(1, nx))
     direct = [tree_sum([dbox[64 * k + j] for j in range(64)]) for k in range(nx - 1)]
     for k in range(nx - 1):
         carry = carry + jnp.where(low & (k < gx), direct[k], 0.0)
@@ -448,11 +445,9 @@
     def _():
         next_copy(0).wait_send()
 
-    total_waits(lambda copy: copy.wait_send(), 4, lambda k: k > gx, lambda k: k > gz)
-    for k in range(1, nx):
-        @pl.when(k > gx)
-        def _():
-            to_device(dbox.at[0:32], dbox.at[0:32], d_send.at[k], d_recv.at[0], g, s ^ 1).wait_send()
+    total_count = later_high + jnp.where(low, 3 - gz, 0)
+    wait_for(sent, lambda k: gbox.at[0:k], g_send, g_recv, total_count, range(1, 4 * nx + 4))
+    wait_for(sent, lambda k: dbox.at[0 : 32 * k], d_send, d_recv, nx - 1 - gx, range(1, nx))
 
 
 def finish(track_in, gene_in, track, gene):
@@ -506,7 +501,7 @@
             pltpu.VMEM((104, LANES), F32),
             pltpu.VMEM((4, 104, LANES), F32),
             pltpu.VMEM((224, 256), BF16),
-            dma((8,)), dma((5,)), dma, dma((4,)), dma, dma, dma((ng // 8 + 8,)), dma((ng // 8 + 8,)), dma((ng // 8,)), dma((ng // 8,)), dma, dma, dma, dma, dma,
+            dma((8,)), dma((5,)), dma, dma((4,)), dma, dma, dma, dma, dma, dma, dma, dma, dma, dma, dma,
             pltpu.SemaphoreType.REGULAR, pltpu.SemaphoreType.REGULAR, pltpu.SemaphoreType.REGULAR,
         ],
         compiler_params=pltpu.CompilerParams(collective_id=0, has_side_effects=True),

time: 18.8 us -> 18.5 us (0.984)
  Pallas kernels: 18 us -> 17.8 us
    pallas_call x1, Pallas kernels: 17.4 us -> 17.2 us  [local(): pl.pallas_call(functools.partial(kernel, ng, samples ** (-0.5), variants...]
where the time goes in v5:
time: 18.5 us; the launch traced here: 18.4 us
  Pallas kernels  17.8 us (96%)
  between operations  0.64 us (3%)
    pallas_call x1, Pallas kernels, local(): pl.pallas_call(functools.partial(kernel, ng, samples ** (-0.5), variants...  17.2 us
    pallas_call x1, Pallas kernels, finished(): pl.pallas_call(finish, out_shape=(jax.ShapeDtypeStruct(track.shape, F32),...  0.64 us

profile of v5, /device:TPU:6, one launch (start us, length us, event | category | flops | bytes accessed | tf_op | source)
XLA Modules:
  0.0 18.4 jit_solution(7427370523151184530)
XLA Ops:
  0.6 17.2 %burden.1 = (f32[64,192]{1,0:T(8,128)S(1)}, f32[16,64]{1,0:T(8,128)S(1)}) custom-call(s32[1024,1536]{1,0:T(8,128)} %geno.1, bf16[64,1024]{1,0:T(8,128)(2,1)} %bitcast.3, s32[12,128]{1,0:T(8,128)} %bitcast.4, f32[8]{0:T(128)} %cweight.1, s32[16]{0:T(128)} %gstart.1, s32[16]{0:T(128)} %gend.1), custom_call_target="tpu_custom_call" | custom-call | tf_op jit(solution)/shard_map/burden/pallas_call | solution.py:478
  17.8 0.6 %finish.1 = (f32[64,192]{1,0:T(8,128)}, f32[16,64]{1,0:T(8,128)}) custom-call(f32[64,192]{1,0:T(8,128)S(1)} %get-tuple-element.6.track_in, f32[16,64]{1,0:T(8,128)S(1)} %get-tuple-element.7.gene_in), custom_call_target="tpu_custom_call" | custom-call | tf_op jit(solution)/shard_map/finish/pallas_call | solution.py:460

commit v6 on v5

--- a/solution.py
+++ b/solution.py
@@ -110,16 +110,17 @@
     for copy in loads[3:]:
         copy.start()
 
-    def tell(group, chip_list):
+    def tell(group, chip_list, side=0):
         for chip in chip_list:
-            pl.semaphore_signal(barrier, inc=1, device_id=(group, 2 * chip), device_id_type=MESH)
+            pl.semaphore_signal(barrier, inc=1, device_id=(group, 2 * chip + side), device_id_type=MESH)
 
     @pl.when(low)
     def _():
         @pl.loop(0, gx)
-        def _(row):
+        def _(back):
             for place in range(7, -1, -1):
-                tell(8 * row + place, range(4))
+                side = jnp.where(gz < 2, 1, 0) if place >= 4 else 0
+                tell(8 * (gx - 1 - back) + place, range(4), side)
 
         @pl.loop(0, gz)
         def _(place):
@@ -142,8 +143,9 @@
                 tell(8 * row + place, [y])
 
     later_high = (nx - 1 - gx) * 4 + jnp.where(low, 4, 7 - gz)
-    group_count = 7 + jnp.where(last_group, 0, 1)
-    far_count = 32 * (nx - 1 - gx) + 2 * jnp.where(low, 3 - gz, 4 * (gx + 1) + 4 * gx + gz - 4)
+    rows_after = nx - 1 - gx
+    group_count = 7 + jnp.where(last_group, 0, 1) + jnp.where(low, 0, 16 * rows_after)
+    far_count = jnp.where(low, 32 * rows_after + 2 * (3 - gz), 16 * rows_after + 2 * (8 * gx + gz))
 
     lane = lax.broadcasted_iota(jnp.int32, (8, LANES), 1)
     sub = lax.broadcasted_iota(jnp.int32, (8, LANES), 0)
@@ -247,6 +249,15 @@
         def _():
             pl.semaphore_wait(group_sem, 1)
 
+    def even_knows_groups():
+        @pl.when(far_count > 0)
+        def _():
+            pl.semaphore_wait(barrier, far_count)
+
+        pl.semaphore_signal(far_sem, inc=1, device_id=(g, 2 * y + 1), device_id_type=MESH)
+
+    known_early = ~low & (gx >= nx // 2)
+
     totals = jnp.zeros((8, LANES), F32)
     pending = None
     for k in range(5):
@@ -260,6 +271,11 @@
             pair_copy(0).start()
         if k >= 2:
             pair_copy(k - 1).start()
+        if k == 3:
+            @pl.when(known_early & ~odd)
+            def _():
+                even_knows_groups()
+
         pending = result
     running = jnp.zeros((1, LANES), F32)
     for k in range(8):
@@ -288,19 +304,6 @@
     def sent(copy):
         copy.wait_send()
 
-    def chip_knows_groups():
-        @pl.when(~odd)
-        def _():
-            @pl.when(far_count > 0)
-            def _():
-                pl.semaphore_wait(barrier, far_count)
-
-            pl.semaphore_signal(far_sem, inc=1, device_id=(g, 2 * y + 1), device_id_type=MESH)
-
-        @pl.when(odd)
-        def _():
-            pl.semaphore_wait(far_sem, 1)
-
     def direct_sends(place):
         @pl.loop(gx + 1, nx)
         def _(row):
@@ -308,8 +311,10 @@
                 slot = 64 * gx + 8 * gz + s
                 to_device(gsum, dbox.at[slot], d_send, d_recv, 8 * row + place, d).start()
 
-    def all_direct_sends():
-        chip_knows_groups()
+    def answers():
+        @pl.when(odd)
+        def _():
+            pl.semaphore_wait(far_sem, 1)
 
         @pl.when(~low)
         def _():
@@ -317,15 +322,14 @@
             def _(other):
                 pl.semaphore_signal(late_sem, inc=1, device_id=(other, s), device_id_type=MESH)
 
-        @pl.loop(0, 4)
-        def _(place):
-            direct_sends(place)
-
-    sends_first = ~low & (gx >= nx // 2)
-
-    @pl.when(sends_first)
-    def _():
-        all_direct_sends()
+    @pl.when(~low)
+    def _():
+        direct_sends(0)
+        direct_sends(1)
+
+    @pl.when(known_early)
+    def _():
+        answers()
 
     to_next = odd & ~last_group
 
@@ -342,9 +346,17 @@
         def _():
             next_copy(k).start()
 
-    @pl.when(~sends_first)
-    def _():
-        all_direct_sends()
+    @pl.when(~known_early)
+    def _():
+        @pl.when(~odd)
+        def _():
+            even_knows_groups()
+
+        answers()
+
+    @pl.loop(jnp.where(low, 0, 2), 4)
+    def _(place):
+        direct_sends(place)
 
     to_device(cbox, cbox, c_send, c_recv, g, s ^ 1).wait_recv()
     group_total = running

time: 18.5 us -> 17.9 us (0.968)
  the two profiles are of different devices: /device:TPU:6 before, /device:TPU:230 now
where the time goes in v6:
time: 17.9 us; the launch traced here: 17.8 us
  Pallas kernels  17.2 us (96%)
  between operations  0.64 us (4%)
    pallas_call x1, Pallas kernels, local(): pl.pallas_call(functools.partial(kernel, ng, samples ** (-0.5), variants...  16.6 us
    pallas_call x1, Pallas kernels, finished(): pl.pallas_call(finish, out_shape=(jax.ShapeDtypeStruct(track.shape, F32),...  0.64 us

profile of v6, /device:TPU:230, one launch (start us, length us, event | category | flops | bytes accessed | tf_op | source)
XLA Modules:
  0.0 17.8 jit_solution(16138477283485677877)
XLA Ops:
  0.6 16.6 %burden.1 = (f32[64,192]{1,0:T(8,128)S(1)}, f32[16,64]{1,0:T(8,128)S(1)}) custom-call(s32[1024,1536]{1,0:T(8,128)} %geno.1, bf16[64,1024]{1,0:T(8,128)(2,1)} %bitcast.3, s32[12,128]{1,0:T(8,128)} %bitcast.4, f32[8]{0:T(128)} %cweight.1, s32[16]{0:T(128)} %gstart.1, s32[16]{0:T(128)} %gend.1), custom_call_target="tpu_custom_call" | custom-call | tf_op jit(solution)/shard_map/burden/pallas_call | solution.py:490
  17.2 0.6 %finish.1 = (f32[64,192]{1,0:T(8,128)}, f32[16,64]{1,0:T(8,128)}) custom-call(f32[64,192]{1,0:T(8,128)S(1)} %get-tuple-element.6.track_in, f32[16,64]{1,0:T(8,128)S(1)} %get-tuple-element.7.gene_in), custom_call_target="tpu_custom_call" | custom-call | tf_op jit(solution)/shard_map/finish/pallas_call | solution.py:472

commit v7 on v6

--- a/solution.py
+++ b/solution.py
@@ -383,7 +383,7 @@
                 def _():
                     total_copy(later).start()
 
-    @pl.when(~low)
+    @pl.when(gz >= 2)
     def _():
         sends_to_late()
 
@@ -410,7 +410,7 @@
     zero = jnp.zeros((16, LANES), F32)
     quad = jnp.where(pick_f, block[96:97], zero) + jnp.where(pick_h, block[97:98], zero)
 
-    @pl.when(low)
+    @pl.when(gz < 2)
     def _():
         sends_to_late()
 

time: 17.9 us -> 17.6 us (0.983)
  the two profiles are of different devices: /device:TPU:230 before, /device:TPU:6 now
where the time goes in v7:
time: 17.6 us; the launch traced here: 17.5 us
  Pallas kernels  16.8 us (95%)
  between operations  0.64 us (4%)
    pallas_call x1, Pallas kernels, local(): pl.pallas_call(functools.partial(kernel, ng, samples ** (-0.5), variants...  16.2 us
    pallas_call x1, Pallas kernels, finished(): pl.pallas_call(finish, out_shape=(jax.ShapeDtypeStruct(track.shape, F32),...  0.64 us

profile of v7, /device:TPU:6, one launch (start us, length us, event | category | flops | bytes accessed | tf_op | source)
XLA Modules:
  0.0 17.5 jit_solution(4866166801752007216)
XLA Ops:
  0.6 16.2 %burden.1 = (f32[64,192]{1,0:T(8,128)S(1)}, f32[16,64]{1,0:T(8,128)S(1)}) custom-call(s32[1024,1536]{1,0:T(8,128)} %geno.1, bf16[64,1024]{1,0:T(8,128)(2,1)} %bitcast.3, s32[12,128]{1,0:T(8,128)} %bitcast.4, f32[8]{0:T(128)} %cweight.1, s32[16]{0:T(128)} %gstart.1, s32[16]{0:T(128)} %gend.1), custom_call_target="tpu_custom_call" | custom-call | tf_op jit(solution)/shard_map/burden/pallas_call | solution.py:490
  16.8 0.6 %finish.1 = (f32[64,192]{1,0:T(8,128)}, f32[16,64]{1,0:T(8,128)}) custom-call(f32[64,192]{1,0:T(8,128)S(1)} %get-tuple-element.6.track_in, f32[16,64]{1,0:T(8,128)S(1)} %get-tuple-element.7.gene_in), custom_call_target="tpu_custom_call" | custom-call | tf_op jit(solution)/shard_map/finish/pallas_call | solution.py:472

commit v8 on v7

--- a/solution.py
+++ b/solution.py
@@ -79,14 +79,14 @@
     for copy in small:
         copy.start()
     chips = [(y + step) % 4 for step in CHIP_STEPS]
-    rows_half = geno.shape[0] // 2
     loads = []
     for k in range(4):
         at = pl.multiple_of(chips[k] * cols, LANES)
-        for h in range(2):
-            rows = slice(h * rows_half, (h + 1) * rows_half)
+        for first_part, parts in ((0, 2), (2, 2)) if k < 3 else ((0, 2), (2, 1), (3, 1)):
+            rows = slice(first_part * 256, (first_part + parts) * 256)
             loads.append(pltpu.make_async_copy(
-                geno.at[rows, pl.ds(at, cols)], gbuf.at[k, rows], load_sem.at[2 * k + h]))
+                geno.at[rows, pl.ds(at, cols)], gbuf.at[k, rows], load_sem.at[len(loads)]))
+
     for copy in loads[:3]:
         copy.start()
 
@@ -202,6 +202,8 @@
         for part in range(4):
             if part % 2 == 0:
                 loads[2 * k + part // 2].wait()
+            elif k == 3 and part == 3:
+                loads[8].wait()
             at = 256 * part
             dose = gbuf[k, at : at + 256, :].astype(F32)
             dose = dose.astype(BF16)
@@ -462,18 +464,26 @@
     wait_for(sent, lambda k: dbox.at[0 : 32 * k], d_send, d_recv, nx - 1 - gx, range(1, nx))
 
 
-def finish(track_in, gene_in, track, gene):
-    track[...] = track_in[...]
-    gene[...] = gene_in[...]
+def finish(track_in, gene_in, track, gene, sem):
+    copies = [
+        pltpu.make_async_copy(track_in, track, sem.at[0]),
+        pltpu.make_async_copy(gene_in, gene, sem.at[1]),
+    ]
+    for copy in copies:
+        copy.start()
+    for copy in copies:
+        copy.wait()
 
 
 def finished(track, gene):
     vmem = pl.BlockSpec(memory_space=pltpu.VMEM)
+    anywhere = pl.BlockSpec(memory_space=pl.ANY)
     track, gene = pl.pallas_call(
         finish,
         out_shape=(jax.ShapeDtypeStruct(track.shape, F32), jax.ShapeDtypeStruct(gene.shape, F32)),
         in_specs=[vmem, vmem],
-        out_specs=(vmem, vmem),
+        out_specs=(anywhere, anywhere),
+        scratch_shapes=[pltpu.SemaphoreType.DMA((2,))],
         compiler_params=pltpu.CompilerParams(vmem_limit_bytes=1 << 20),
         name="finish",
     )(track, gene)
@@ -513,7 +523,7 @@
             pltpu.VMEM((104, LANES), F32),
             pltpu.VMEM((4, 104, LANES), F32),
             pltpu.VMEM((224, 256), BF16),
-            dma((8,)), dma((5,)), dma, dma((4,)), dma, dma, dma, dma, dma, dma, dma, dma, dma, dma, dma,
+            dma((9,)), dma((5,)), dma, dma((4,)), dma, dma, dma, dma, dma, dma, dma, dma, dma, dma, dma,
             pltpu.SemaphoreType.REGULAR, pltpu.SemaphoreType.REGULAR, pltpu.SemaphoreType.REGULAR,
         ],
         compiler_params=pltpu.CompilerParams(collective_id=0, has_side_effects=True),

time: 17.6 us -> 17.6 us (level)
  no operation moved by 1% of the time
where the time goes in v8:
time: 17.6 us
  Pallas kernels  16.9 us (96%)
  between operations  0.64 us (4%)
    pallas_call x1, Pallas kernels, local(): pl.pallas_call(functools.partial(kernel, ng, samples ** (-0.5), variants...  16.3 us
    pallas_call x1, Pallas kernels, finished(): pl.pallas_call(finish, out_shape=(jax.ShapeDtypeStruct(track.shape, F32),...  0.65 us

profile of v8, /device:TPU:6, one launch (start us, length us, event | category | flops | bytes accessed | tf_op | source)
XLA Modules:
  0.0 17.6 jit_solution(3600249043781995822)
XLA Ops:
  0.6 16.3 %burden.1 = (f32[64,192]{1,0:T(8,128)S(1)}, f32[16,64]{1,0:T(8,128)S(1)}) custom-call(s32[1024,1536]{1,0:T(8,128)} %geno.1, bf16[64,1024]{1,0:T(8,128)(2,1)} %bitcast.3, s32[12,128]{1,0:T(8,128)} %bitcast.4, f32[8]{0:T(128)} %cweight.1, s32[16]{0:T(128)} %gstart.1, s32[16]{0:T(128)} %gend.1), custom_call_target="tpu_custom_call" | custom-call | tf_op jit(solution)/shard_map/burden/pallas_call | solution.py:500
  16.9 0.7 %finish.1 = (f32[64,192]{1,0:T(8,128)}, f32[16,64]{1,0:T(8,128)}) custom-call(f32[64,192]{1,0:T(8,128)S(1)} %get-tuple-element.6.track_in, f32[16,64]{1,0:T(8,128)S(1)} %get-tuple-element.7.gene_in), custom_call_target="tpu_custom_call" | custom-call | tf_op jit(solution)/shard_map/finish/pallas_call | solution.py:481
